TPU v7x, 128 devices: a whole 4x4x4 slice. The times are simulated.
128 devices in a mesh: band: 8 (over y, x_lo), chan: 16 (over x_hi, z, core).
Axes of the slice: x: 4 (x_hi: 2, x_lo: 2; x = x_hi * 2 + x_lo), y: 4, z: 4, core: 2. Of those that a mesh axis runs over, the one named last changes fastest.
Arguments:
- coeffs: bfloat16 [2, 8, 1024, 8192], P(None, None, 'chan', 'band'), may hold values from -1100 to 1100, as said below
Outputs:
- coherence: float32 [1024, 1024], P('chan', 'band')
Inputs may be any that keep to these rules, and one draw needn't show every extreme that they name: `coeffs`: finite real and imaginary parts.
All inputs are finite; a program needn't handle non-finite values.
Results may differ from a plain program's by a relative error of at most 0.0003.
Values may be sent and summed in bfloat16 or wider, within the bound.
A program may use at most 192 MiB of HBM per device.

v0:
```python
import functools

import jax
import jax.numpy as jnp
from jax import lax
from jax.experimental import pallas as pl
from jax.experimental.pallas import tpu as pltpu
from jax.sharding import PartitionSpec as P

W = 16

epsilon = 1e-06

MESH = pl.DeviceIdType.MESH


def partner(index, size, offset):
    other = index
    bit = 1
    while bit < size:
        if offset & bit:
            other = other + (1 - 2 * ((index // bit) % 2)) * bit
        bit *= 2
    return other


def kernel(x_ref, out_ref, buf, sel, xb, xq, inv_col, inv_row, own_sem, send_sem, recv_sem):
    n = lax.axis_size("chan")
    me = lax.axis_index("chan")
    parts, tapers, own, wide = buf.shape[1:]
    bands, full, depth = xb.shape
    lanes = bands * W
    half = depth // 2
    tile = min(256, full)

    def window(device):
        return pl.ds(pl.multiple_of(device * lanes // wide * wide, wide), wide)

    barrier = pltpu.get_barrier_semaphore()
    for offset in range(1, n):
        pl.semaphore_signal(
            barrier, inc=1, device_id={"chan": partner(me, n, offset)}, device_id_type=MESH
        )

    local = pltpu.make_async_copy(
        x_ref.at[:, :, :, window(me)], buf.at[me], own_sem
    )
    local.start()
    pl.semaphore_wait(barrier, n - 1)

    copies = {}
    for offset in reversed(range(1, n)):
        peer = partner(me, n, offset)
        copies[offset] = pltpu.make_async_remote_copy(
            src_ref=x_ref.at[:, :, :, window(peer)],
            dst_ref=buf.at[me],
            send_sem=send_sem.at[offset],
            recv_sem=recv_sem.at[offset],
            device_id={"chan": peer},
            device_id_type=MESH,
        )
        copies[offset].start()

    row = lax.broadcasted_iota(jnp.int32, (wide, bands * half), 0) - (me * lanes) % wide
    col = lax.broadcasted_iota(jnp.int32, (wide, bands * half), 1)
    band, within = col // half, col % half
    for k in range(tapers):
        hit = (row == band * W + within - k * W) & (within // W == k)
        sel[k * wide : (k + 1) * wide, :] = jnp.where(hit, 1.0, 0.0).astype(jnp.bfloat16)

    def relayout(src):
        rows = pl.ds(pl.multiple_of(src * own, own), own)
        re = jnp.concatenate([buf[src, 0, k] for k in range(tapers)], axis=1)
        im = jnp.concatenate([buf[src, 1, k] for k in range(tapers)], axis=1)
        lane = lax.broadcasted_iota(jnp.int32, (own, 128), 1)
        power = jnp.ones((own, 128), jnp.float32)
        for b in range(bands):
            chosen = sel[:, b * half : (b + 1) * half]
            re_b = jnp.dot(re, chosen, preferred_element_type=jnp.float32)
            im_b = jnp.dot(im, chosen, preferred_element_type=jnp.float32)
            total = jnp.sum(re_b * re_b + im_b * im_b, axis=1, keepdims=True) + epsilon
            power = jnp.where(lane == b, total, power)
            xb[b, rows, :half] = re_b.astype(jnp.bfloat16)
            xb[b, rows, half:] = im_b.astype(jnp.bfloat16)
            xq[b, rows, :half] = im_b.astype(jnp.bfloat16)
            xq[b, rows, half:] = (-re_b).astype(jnp.bfloat16)
        inv_col[rows, :] = 1.0 / power

    local.wait()
    relayout(me)
    for offset in range(1, n):
        copies[offset].wait_recv()
        relayout(partner(me, n, offset))

    count = full // tile
    for i in range(count):
        turned = inv_col[i * tile : (i + 1) * tile, :].T
        inv_row[:, i * tile : (i + 1) * tile] = turned[:bands, :]

    contract = (((1,), (1,)), ((), ()))
    for i in range(count):
        row0 = i * tile

        def column(j, carry):
            col0 = pl.multiple_of(j * tile, tile)
            acc = jnp.zeros((tile, tile), jnp.float32)
            for b in range(bands):
                right = xb[b, pl.ds(col0, tile), :]
                re = lax.dot_general(
                    xb[b, row0 : row0 + tile, :], right, contract, preferred_element_type=jnp.float32
                )
                im = lax.dot_general(
                    xq[b, row0 : row0 + tile, :], right, contract, preferred_element_type=jnp.float32
                )
                acc += ((re * re + im * im) * inv_col[row0 : row0 + tile, b : b + 1]) * inv_row[
                    b : b + 1, pl.ds(col0, tile)
                ]
            out_ref[row0 : row0 + tile, pl.ds(col0, tile)] = acc
            out_ref[pl.ds(col0, tile), row0 : row0 + tile] = acc.T
            return carry

        lax.fori_loop(i, count, column, 0)

    for offset in range(1, n):
        copies[offset].wait_send()


def body(coeffs):
    parts, tapers, own, bins = coeffs.shape
    n = lax.axis_size("chan")
    groups = lax.axis_size("band")
    full = own * n
    lanes = bins // n
    wide = max(lanes, 128)
    bands = lanes // W
    depth = parts * tapers * W
    scale = jnp.float32(W * tapers / (bins // W * groups))
    partial_sum = pl.pallas_call(
        kernel,
        out_shape=jax.ShapeDtypeStruct((full, full), jnp.float32),
        in_specs=[pl.BlockSpec(memory_space=pl.ANY)],
        out_specs=pl.BlockSpec(memory_space=pltpu.VMEM),
        scratch_shapes=[
            pltpu.VMEM((n, parts, tapers, own, wide), jnp.bfloat16),
            pltpu.VMEM((tapers * wide, bands * tapers * W), jnp.bfloat16),
            pltpu.VMEM((bands, full, depth), jnp.bfloat16),
            pltpu.VMEM((bands, full, depth), jnp.bfloat16),
            pltpu.VMEM((full, 128), jnp.float32),
            pltpu.VMEM((bands, full), jnp.float32),
            pltpu.SemaphoreType.DMA,
            pltpu.SemaphoreType.DMA((n,)),
            pltpu.SemaphoreType.DMA((n,)),
        ],
        compiler_params=pltpu.CompilerParams(
            collective_id=0, has_side_effects=True, vmem_limit_bytes=48 * 1024 * 1024
        ),
    )(coeffs)
    summed = lax.psum_scatter(partial_sum, "band", scatter_dimension=1, tiled=True)
    summed = lax.psum_scatter(summed, "chan", scatter_dimension=0, tiled=True)
    share = full // groups
    row_global = lax.broadcasted_iota(jnp.int32, (own, share), 0) + lax.axis_index("chan") * own
    col_global = lax.broadcasted_iota(jnp.int32, (own, share), 1) + lax.axis_index("band") * share
    return jnp.where(row_global == col_global, jnp.float32(0.0), summed) * scale


def solution(mesh):
    return jax.shard_map(
        body,
        mesh=mesh,
        in_specs=(P(None, None, "chan", "band"),),
        out_specs=P("chan", "band"),
        check_vma=False,
    )
```

profile of v0, /device:TPU:0, one launch (start us, length us, event | category | flops | bytes accessed | tf_op | source)
XLA Modules:
  0.0 255.0 jit_solution(9522812697330738888)
XLA Ops:
  6.5 0.0 reduce-scatter.3.cloned.1.call-start
  6.5 0.0 copy-start
  6.5 1.6 copy-done
  8.1 79.5 %shard_map.17 = f32[1024,1024]{1,0:T(8,128)} custom-call(bf16[2,8,64,1024]{3,2,1,0:T(8,128)(2,1)S(1)} %copy-done), custom_call_target="tpu_custom_call" | custom-call | tf_op jit(solution)/shard_map/pallas_call | solution.py:138
  87.7 0.0 reduce-scatter.3.cloned.1.call-update
  87.7 0.0 reduce-scatter.5.cloned.1.call-start
  87.7 89.5 %reduce-scatter.3.cloned.1.call-done = f32[1024,128]{1,0:T(8,128)} async-done(((f32[1024,1024]{1,0:T(8,128)}), f32[1024,128]{1,0:T(8,128)}) %reduce-scatter.3.cloned.1.call-update) | async-done | bytes 524304 | tf_op jit(solution)/shard_map/reduce_scatter | solution.py:158
  177.2 0.0 reduce-scatter.5.cloned.1.call-update
  177.3 69.4 %reduce-scatter.5.cloned.1.call-done = f32[64,128]{1,0:T(8,128)} async-done(((f32[1024,128]{1,0:T(8,128)}), f32[64,128]{1,0:T(8,128)}) %reduce-scatter.5.cloned.1.call-update) | async-done | bytes 32784 | tf_op jit(solution)/shard_map/reduce_scatter | solution.py:159
  246.7 1.4 select_multiply_fusion
  (2 shorter events, 0.0 us)
Async XLA Ops:
  6.5 170.7 %reduce-scatter.3.cloned.1.call-start = ((), (), s32[]{:S(2)}) async-start(), calls=%async_computation.2 | async-start | bytes 4718592 | tf_op jit(solution)/shard_map/reduce_scatter | solution.py:158
  6.5 1.6 copy-start
  87.7 159.0 %reduce-scatter.5.cloned.1.call-start = ((), (), s32[]{:S(2)}) async-start(), calls=%async_computation.3 | async-start | bytes 557056 | tf_op jit(solution)/shard_map/reduce_scatter | solution.py:159
Sparse Core Ops, SparseCore 0:
  87.8 89.3 reduce-scatter.2
  180.9 65.7 reduce-scatter.4
where the time goes:
time: 255 us
  waiting for transfers between devices  159 us (62%)
  Pallas kernels  79.5 us (31%)
  between operations  13.4 us (5%)
    reduce_scatter x1, waiting for transfers between devices, body(): lax.psum_scatter(partial_sum, 'band', scatter_dimension=1, tiled=True)  89.5 us
    pallas_call x1, Pallas kernels, body(): pl.pallas_call(kernel, out_shape=jax.ShapeDtypeStruct((full, full), jnp.f...  79.5 us
    reduce_scatter x1, waiting for transfers between devices, body(): summed = lax.psum_scatter(summed, 'chan', scatter_dimension=0, tiled=True)  69.4 us
  transfers between devices with their start and end apart: 2, of which 2 were waited for; matrix products, arithmetic and copies ran while one was open for 0% of the time, Pallas kernels for 0%

commit v1 on v0

v1 whole, which is shorter than its diff:
```python
import jax
import jax.numpy as jnp
from jax import lax
from jax.experimental import pallas as pl
from jax.experimental.pallas import tpu as pltpu
from jax.sharding import PartitionSpec as P

W = 16
CHUNKS = 2

epsilon = 1e-06

MESH = pl.DeviceIdType.MESH

PARTS = ((0, 24, "xyz"), (24, 48, "yzx"), (48, 64, "zxy"))


def kernel(
    x_ref, out_ref, win, snd, xb, inv_col, inv_row, pa, pb, pc, ra1, rb1, rc1, ra2, rb2, rc2, ra3, rb3, rc3,
    load_sem, send_sem, recv_sem, pass_sem, passed_sem, out_sem, in_sem,
):
    band = lax.axis_index("band")
    chan = lax.axis_index("chan")
    core = chan % 2
    z = (chan // 2) % 4
    x_hi = chan // 8
    y = band // 2
    x = x_hi * 2 + band % 2
    me = x_hi * 4 + z
    bands, chips, cores, own, depth = xb.shape
    half = depth // 2
    tapers = half // W
    step = bands // CHUNKS

    def device(x, y, z, core):
        return {"band": y * 2 + x % 2, "chan": ((x // 2) * 4 + z) * 2 + core}

    def to_chip(i):
        return ((x_hi + i // 4) % 2) * 4 + (z + i % 4) % 4

    def from_chip(i):
        return ((x_hi + 2 - i // 4) % 2) * 4 + (z + 4 - i % 4) % 4

    def same_group(chip):
        return {"band": band, "chan": chip * 2 + core}

    sibling = {"band": band, "chan": me * 2 + 1 - core}

    barrier = pltpu.get_barrier_semaphore()
    peers = [same_group(to_chip(i)) for i in range(1, 8)] + [sibling]
    peers += [device((x + o) % 4, y, z, core) for o in (1, 3)]
    peers += [device(x, (y + o) % 4, z, core) for o in (1, 2, 3)]
    for peer in peers:
        pl.semaphore_signal(barrier, inc=1, device_id=peer, device_id_type=MESH)

    def load(i):
        chip = to_chip(i)
        lanes = pl.ds(pl.multiple_of(chip * 128, 128), 128)
        return pltpu.make_async_copy(x_ref.at[:, :, :, lanes], win.at[i], load_sem.at[i])

    for i in range(chips):
        load(i).start()

    lane_band = lax.broadcasted_iota(jnp.int32, (16, 128), 1) // W

    def transposed(i, put):
        for part in range(2):
            for r in range(0, own, 16):
                v = [win[i, part, k, r : r + 16, :].astype(jnp.float32) for k in range(tapers)]
                bit = 1
                while bit < tapers:
                    upper = (lane_band // bit) % 2 == 1
                    for a in range(tapers):
                        if not a & bit:
                            b = a | bit
                            up = pltpu.roll(v[b], W * bit, 1)
                            down = pltpu.roll(v[a], 128 - W * bit, 1)
                            v[a], v[b] = jnp.where(upper, up, v[a]), jnp.where(upper, v[b], down)
                    bit *= 2
                for b in range(bands):
                    put(b, r, part, v[b].astype(jnp.bfloat16))

    load(0).wait()

    def put_own(b, r, part, value):
        xb[b, me, core, r : r + 16, part * half : (part + 1) * half] = value

    transposed(0, put_own)

    def relayout(j, carry):
        i = chips - 1 - j
        load(i).wait()

        def put(b, r, part, value):
            snd[i, b, r : r + 16, part * half : (part + 1) * half] = value

        transposed(i, put)
        return carry

    lax.fori_loop(0, chips - 1, relayout, 0)

    def send(i, c):
        return pltpu.make_async_remote_copy(
            src_ref=snd.at[i, pl.ds(c * step, step)],
            dst_ref=xb.at[pl.ds(c * step, step), me, core],
            send_sem=send_sem.at[i, c],
            recv_sem=recv_sem.at[i, c],
            device_id=same_group(to_chip(i)),
            device_id_type=MESH,
        )

    def forward(i, c):
        chip = from_chip(i)
        return pltpu.make_async_remote_copy(
            src_ref=xb.at[pl.ds(c * step, step), chip, core],
            dst_ref=xb.at[pl.ds(c * step, step), chip, core],
            send_sem=pass_sem.at[i, c],
            recv_sem=passed_sem.at[i, c],
            device_id=sibling,
            device_id_type=MESH,
        )

    pl.semaphore_wait(barrier, len(peers))
    for c in range(CHUNKS):
        def start_send(j, carry):
            send(chips - 1 - j, c).start()
            return carry

        lax.fori_loop(0, chips - 1, start_send, 0)
        forward(0, c).start()

    lane = lax.broadcasted_iota(jnp.int32, (2 * own, 128), 1)

    def normalise(i, c):
        forward(i, c).wait_recv()
        chip = from_chip(i)
        power = jnp.ones((2 * own, 128), jnp.float32)
        for b in range(step):
            v = xb[c * step + b, chip].reshape(2 * own, depth).astype(jnp.float32)
            v = v * v
            total = jnp.sum(v[:, :half] + v[:, half:], axis=1, keepdims=True) + epsilon
            power = jnp.where(lane == b, total, power)
        inverse = 1.0 / power
        inv_col[c, pl.ds(pl.multiple_of(chip * 2 * own, 128), 2 * own), :] = inverse
        inv_row[c, :, pl.ds(pl.multiple_of(chip * 128, 128), 128)] = inverse.T[:8, :]

    contract = (((1,), (1,)), ((), ()))
    stores = ((pa, 0), (pb, 1), (pc, 2))

    for c in range(CHUNKS):
        def arrive(j, carry):
            i = chips - 1 - j
            send(i, c).wait_recv()
            forward(i, c).start()
            normalise((i + 1) % chips, c)
            return carry

        lax.fori_loop(0, chips - 1, arrive, 0)
        normalise(1, c)

        def tile(t, carry):
            row = t // 4
            col = t % 4
            acc = jnp.zeros((256, 256), jnp.float32)
            scale_row = inv_row[c, :, pl.ds(pl.multiple_of(col * 256, 256), 256)]
            for b in range(step):
                left = xb[c * step + b, pl.ds(row * 4, 4), core].reshape(256, depth)
                right = xb[c * step + b, pl.ds(col * 2, 2)].reshape(256, depth)
                turned = jnp.concatenate([left[:, half:], -left[:, :half]], axis=1)
                re = lax.dot_general(left, right, contract, preferred_element_type=jnp.float32)
                im = lax.dot_general(turned, right, contract, preferred_element_type=jnp.float32)
                rows = jnp.concatenate(
                    [
                        inv_col[c, pl.ds(pl.multiple_of((row * 4 + q) * 128 + core * own, own), own), b : b + 1]
                        for q in range(4)
                    ],
                    axis=0,
                )
                acc += ((re * re + im * im) * rows) * scale_row[b : b + 1, :]
            for q in range(4):
                for s in range(2):
                    for ref, n in stores:
                        low, high, order = PARTS[n]
                        at = {"x": row * 2 + s, "y": col, "z": q}
                        index = tuple(at[d] for d in order)
                        value = acc[q * 64 + low : q * 64 + high, s * 128 : (s + 1) * 128]
                        if c > 0:
                            value = value + ref[index]
                        ref[index] = value
            return carry

        lax.fori_loop(0, 8, tile, 0)

    at = {"x": x, "y": y, "z": z}

    def hop(n, phase, o):
        low, high, order = PARTS[n]
        dim = order[phase]
        there = dict(at)
        there[dim] = (at[dim] + o) % 4
        src = stores[n][0]
        for d in order[:phase]:
            src = src.at[at[d]]
        return pltpu.make_async_remote_copy(
            src_ref=src.at[there[dim]],
            dst_ref=((ra1, rb1, rc1), (ra2, rb2, rc2), (ra3, rb3, rc3))[phase][n].at[o - 1],
            send_sem=out_sem.at[n, phase, o],
            recv_sem=in_sem.at[n, phase, o],
            device_id=device(there["x"], there["y"], there["z"], core),
            device_id_type=MESH,
        )

    for n in range(3):
        for o in (2, 1, 3):
            hop(n, 0, o).start()
    for phase in range(3):
        for n in range(3):
            low, high, order = PARTS[n]
            got = ((ra1, rb1, rc1), (ra2, rb2, rc2), (ra3, rb3, rc3))[phase][n]
            for o in (1, 3, 2):
                hop(n, phase, o).wait_recv()
            index = tuple(at[d] for d in order[: phase + 1])
            total = (stores[n][0][index] + got[0]) + (got[1] + got[2])
            if phase < 2:
                stores[n][0][index] = total
                for o in (2, 1, 3):
                    hop(n, phase + 1, o).start()
            else:
                groups = lax.axis_size("band")
                scale = jnp.float32(W * tapers / (bands * chips * groups))
                row = lax.broadcasted_iota(jnp.int32, (high - low, 128), 0) + (chan * own + low)
                col = lax.broadcasted_iota(jnp.int32, (high - low, 128), 1) + band * 128
                out_ref[low:high, :] = jnp.where(row == col, jnp.float32(0.0), total) * scale

    for n in range(3):
        for phase in range(3):
            for o in (1, 2, 3):
                hop(n, phase, o).wait_send()
    for c in range(CHUNKS):
        def finish(i, carry):
            send(i, c).wait_send()
            forward(i, c).wait_send()
            return carry

        lax.fori_loop(1, chips, finish, 0)
        forward(0, c).wait_send()


def body(coeffs):
    parts, tapers, own, bins = coeffs.shape
    chips = lax.axis_size("chan") // 2
    bands = 128 // W
    depth = parts * tapers * W
    rows = [high - low for low, high, _ in PARTS]
    f32 = jnp.float32
    bf16 = jnp.bfloat16
    scratch = [
        pltpu.VMEM((chips, parts, tapers, own, 128), bf16),
        pltpu.VMEM((chips, bands, own, depth), bf16),
        pltpu.VMEM((bands, chips, 2, own, depth), bf16),
        pltpu.VMEM((CHUNKS, chips * 2 * own, 128), f32),
        pltpu.VMEM((CHUNKS, 8, chips * 2 * own), f32),
    ]
    scratch += [pltpu.VMEM((4, 4, 4, r, 128), f32) for r in rows]
    scratch += [pltpu.VMEM((3, 4, 4, r, 128), f32) for r in rows]
    scratch += [pltpu.VMEM((3, 4, r, 128), f32) for r in rows]
    scratch += [pltpu.VMEM((3, r, 128), f32) for r in rows]
    scratch += [
        pltpu.SemaphoreType.DMA((chips,)),
        pltpu.SemaphoreType.DMA((chips, CHUNKS)),
        pltpu.SemaphoreType.DMA((chips, CHUNKS)),
        pltpu.SemaphoreType.DMA((chips, CHUNKS)),
        pltpu.SemaphoreType.DMA((chips, CHUNKS)),
        pltpu.SemaphoreType.DMA((3, 3, 4)),
        pltpu.SemaphoreType.DMA((3, 3, 4)),
    ]
    return pl.pallas_call(
        kernel,
        out_shape=jax.ShapeDtypeStruct((own, 128), f32),
        in_specs=[pl.BlockSpec(memory_space=pl.ANY)],
        out_specs=pl.BlockSpec(memory_space=pltpu.VMEM),
        scratch_shapes=scratch,
        compiler_params=pltpu.CompilerParams(
            collective_id=0, has_side_effects=True, vmem_limit_bytes=60 * 1024 * 1024
        ),
    )(coeffs)


def solution(mesh):
    return jax.shard_map(
        body,
        mesh=mesh,
        in_specs=(P(None, None, "chan", "band"),),
        out_specs=P("chan", "band"),
        check_vma=False,
    )
```

time: 255 us -> 65.3 us (0.26)
  waiting for transfers between devices: 159 us -> 0 us
  Pallas kernels: 79.5 us -> 63.7 us
  between operations: 13.4 us -> 0.01 us
    reduce_scatter x2 -> x0, waiting for transfers between devices: 159 us -> none  [the longest x1 89.5 us: body(): lax.psum_scatter(partial_sum, 'band', scatter_dimension=1, tiled=True)]
    pallas_call x1, Pallas kernels: 79.5 us -> 63.7 us  [body(): pl.pallas_call(kernel, out_shape=jax.ShapeDtypeStruct((own, 128), f32), i...]
  transfers between devices with their start and end apart: 2 -> 0, of which waited for: 2 -> 0; matrix products, arithmetic and copies ran while one was open for 0% -> 0% of each run, Pallas kernels for 0% -> 0%
where the time goes in v1:
time: 65.3 us; the launch traced here: 65.1 us
  Pallas kernels  63.7 us (98%)
  local copies, waits for them, and re-layouts  1.38 us (2%)
    pallas_call x1, Pallas kernels, body(): pl.pallas_call(kernel, out_shape=jax.ShapeDtypeStruct((own, 128), f32), i...  63.7 us
    unnamed x1, local copies, waits for them, and re-layouts  1.38 us

profile of v1, /device:TPU:0, one launch (start us, length us, event | category | flops | bytes accessed | tf_op | source)
XLA Modules:
  0.0 65.1 jit_solution(16197379556277677171)
XLA Ops:
  0.0 63.7 %shard_map.17 = f32[64,128]{1,0:T(8,128)} custom-call(bf16[2,8,64,1024]{3,2,1,0:T(8,128)(2,1)} %x_ref.1), custom_call_target="tpu_custom_call" | custom-call | tf_op jit(solution)/shard_map/pallas_call | solution.py:277
  63.8 1.4 %copy.3 = f32[64,128]{1,0:T(8,128)} copy(f32[64,128]{1,0:T(8,128)} %shard_map.17) | data formatting | bytes 65536

commit v2 on v1

--- a/solution.py
+++ b/solution.py
@@ -6,7 +6,7 @@
 from jax.sharding import PartitionSpec as P
 
 W = 16
-CHUNKS = 2
+CHUNKS = 1
 
 epsilon = 1e-06
 
@@ -146,73 +146,86 @@
 
     contract = (((1,), (1,)), ((), ()))
     stores = ((pa, 0), (pb, 1), (pc, 2))
-
-    for c in range(CHUNKS):
-        def arrive(j, carry):
-            i = chips - 1 - j
-            send(i, c).wait_recv()
-            forward(i, c).start()
-            normalise((i + 1) % chips, c)
-            return carry
-
-        lax.fori_loop(0, chips - 1, arrive, 0)
-        normalise(1, c)
-
-        def tile(t, carry):
-            row = t // 4
-            col = t % 4
-            acc = jnp.zeros((256, 256), jnp.float32)
-            scale_row = inv_row[c, :, pl.ds(pl.multiple_of(col * 256, 256), 256)]
-            for b in range(step):
-                left = xb[c * step + b, pl.ds(row * 4, 4), core].reshape(256, depth)
-                right = xb[c * step + b, pl.ds(col * 2, 2)].reshape(256, depth)
-                turned = jnp.concatenate([left[:, half:], -left[:, :half]], axis=1)
-                re = lax.dot_general(left, right, contract, preferred_element_type=jnp.float32)
-                im = lax.dot_general(turned, right, contract, preferred_element_type=jnp.float32)
-                rows = jnp.concatenate(
-                    [
-                        inv_col[c, pl.ds(pl.multiple_of((row * 4 + q) * 128 + core * own, own), own), b : b + 1]
-                        for q in range(4)
-                    ],
-                    axis=0,
-                )
-                acc += ((re * re + im * im) * rows) * scale_row[b : b + 1, :]
-            for q in range(4):
-                for s in range(2):
-                    for ref, n in stores:
-                        low, high, order = PARTS[n]
-                        at = {"x": row * 2 + s, "y": col, "z": q}
-                        index = tuple(at[d] for d in order)
-                        value = acc[q * 64 + low : q * 64 + high, s * 128 : (s + 1) * 128]
-                        if c > 0:
-                            value = value + ref[index]
-                        ref[index] = value
-            return carry
-
-        lax.fori_loop(0, 8, tile, 0)
-
     at = {"x": x, "y": y, "z": z}
 
-    def hop(n, phase, o):
-        low, high, order = PARTS[n]
-        dim = order[phase]
-        there = dict(at)
-        there[dim] = (at[dim] + o) % 4
+    def target(dim, there):
+        place = dict(at)
+        place[dim] = there
+        return device(place["x"], place["y"], place["z"], core)
+
+    def hop(n, phase, o, cut=()):
+        dim = PARTS[n][2][phase]
+        there = (at[dim] + o) % 4
         src = stores[n][0]
-        for d in order[:phase]:
+        for d in PARTS[n][2][:phase]:
             src = src.at[at[d]]
+        src = src.at[there]
+        dst = ((ra1, rb1, rc1), (ra2, rb2, rc2), (ra3, rb3, rc3))[phase][n].at[o - 1]
+        if cut:
+            src, dst = src.at[cut], dst.at[cut]
         return pltpu.make_async_remote_copy(
-            src_ref=src.at[there[dim]],
-            dst_ref=((ra1, rb1, rc1), (ra2, rb2, rc2), (ra3, rb3, rc3))[phase][n].at[o - 1],
+            src_ref=src,
+            dst_ref=dst,
             send_sem=out_sem.at[n, phase, o],
             recv_sem=in_sem.at[n, phase, o],
-            device_id=device(there["x"], there["y"], there["z"], core),
+            device_id=target(dim, there),
             device_id_type=MESH,
         )
 
-    for n in range(3):
-        for o in (2, 1, 3):
-            hop(n, 0, o).start()
+    def follow(j):
+        return (chips - j) % chips
+
+    def arrive(j, carry):
+        i = follow(j)
+        send(i, 0).wait_recv()
+        forward(i, 0).start()
+        normalise(follow(j - 1), 0)
+        return carry
+
+    lax.fori_loop(1, chips, arrive, 0)
+    normalise(1, 0)
+
+    def tile(t, carry):
+        row = (x_hi + 1 + t // 4) % 2
+        col = (y + 2 + 3 * (t % 4)) % 4
+        acc = jnp.zeros((256, 256), jnp.float32)
+        scale_row = inv_row[0, :, pl.ds(pl.multiple_of(col * 256, 256), 256)]
+        for b in range(bands):
+            left = xb[b, pl.ds(row * 4, 4), core].reshape(256, depth)
+            right = xb[b, pl.ds(col * 2, 2)].reshape(256, depth)
+            turned = jnp.concatenate([left[:, half:], -left[:, :half]], axis=1)
+            re = lax.dot_general(left, right, contract, preferred_element_type=jnp.float32)
+            im = lax.dot_general(turned, right, contract, preferred_element_type=jnp.float32)
+            rows = jnp.concatenate(
+                [
+                    inv_col[0, pl.ds(pl.multiple_of((row * 4 + q) * 128 + core * own, own), own), b : b + 1]
+                    for q in range(4)
+                ],
+                axis=0,
+            )
+            acc += ((re * re + im * im) * rows) * scale_row[b : b + 1, :]
+        for q in range(4):
+            for s in range(2):
+                for ref, n in stores:
+                    low, high, order = PARTS[n]
+                    place = {"x": row * 2 + s, "y": col, "z": q}
+                    ref[tuple(place[d] for d in order)] = acc[q * 64 + low : q * 64 + high, s * 128 : (s + 1) * 128]
+        for o in range(1, 4):
+            x_to = (x + o) % 4
+
+            @pl.when(x_to // 2 == row)
+            def _():
+                hop(0, 0, o, (col,)).start()
+
+            @pl.when((y + o) % 4 == col)
+            def _():
+                hop(1, 0, o, (slice(None), pl.ds(row * 2, 2))).start()
+
+            hop(2, 0, o, (pl.ds(row * 2, 2), col)).start()
+        return carry
+
+    lax.fori_loop(0, 8, tile, 0)
+
     for phase in range(3):
         for n in range(3):
             low, high, order = PARTS[n]

time: 65.3 us -> 61.5 us (0.942)
  Pallas kernels: 63.7 us -> 59.9 us
    pallas_call x1, Pallas kernels: 63.7 us -> 59.9 us  [body(): pl.pallas_call(kernel, out_shape=jax.ShapeDtypeStruct((own, 128), f32), i...]
where the time goes in v2:
time: 61.5 us; the launch traced here: 61.3 us
  Pallas kernels  59.9 us (97%)
  local copies, waits for them, and re-layouts  1.38 us (2%)
    pallas_call x1, Pallas kernels, body(): pl.pallas_call(kernel, out_shape=jax.ShapeDtypeStruct((own, 128), f32), i...  59.9 us
    unnamed x1, local copies, waits for them, and re-layouts  1.38 us

profile of v2, /device:TPU:0, one launch (start us, length us, event | category | flops | bytes accessed | tf_op | source)
XLA Modules:
  0.0 61.3 jit_solution(3277870999576914498)
XLA Ops:
  0.0 59.9 %shard_map.17 = f32[64,128]{1,0:T(8,128)} custom-call(bf16[2,8,64,1024]{3,2,1,0:T(8,128)(2,1)} %x_ref.1), custom_call_target="tpu_custom_call" | custom-call | tf_op jit(solution)/shard_map/pallas_call | solution.py:290
  59.9 1.4 %copy.3 = f32[64,128]{1,0:T(8,128)} copy(f32[64,128]{1,0:T(8,128)} %shard_map.17) | data formatting | bytes 65536

commit v3 on v2

--- a/solution.py
+++ b/solution.py
@@ -294,7 +294,7 @@
         out_specs=pl.BlockSpec(memory_space=pltpu.VMEM),
         scratch_shapes=scratch,
         compiler_params=pltpu.CompilerParams(
-            collective_id=0, has_side_effects=True, vmem_limit_bytes=60 * 1024 * 1024
+            collective_id=0, has_side_effects=True, vmem_limit_bytes=54000 * 1024
         ),
     )(coeffs)
 

time: 61.5 us -> 60 us (0.976)
  local copies, waits for them, and re-layouts: 1.38 us -> 0.62 us
    unnamed x1, local copies, waits for them, and re-layouts: 1.38 us -> 0.62 us
where the time goes in v3:
time: 60 us; the launch traced here: 59.9 us
  Pallas kernels  59.3 us (99%)
  local copies, waits for them, and re-layouts  0.62 us (1%)
    pallas_call x1, Pallas kernels, body(): pl.pallas_call(kernel, out_shape=jax.ShapeDtypeStruct((own, 128), f32), i...  59.3 us

profile of v3, /device:TPU:0, one launch (start us, length us, event | category | flops | bytes accessed | tf_op | source)
XLA Modules:
  0.0 59.9 jit_solution(16166502756181961164)
XLA Ops:
  0.0 59.3 %shard_map.17 = f32[64,128]{1,0:T(8,128)S(1)} custom-call(bf16[2,8,64,1024]{3,2,1,0:T(8,128)(2,1)} %x_ref.1), custom_call_target="tpu_custom_call" | custom-call | tf_op jit(solution)/shard_map/pallas_call | solution.py:290
  59.3 0.6 %copy.3 = f32[64,128]{1,0:T(8,128)} copy(f32[64,128]{1,0:T(8,128)S(1)} %shard_map.17) | data formatting | bytes 65536

commit v4 on v3

--- a/solution.py
+++ b/solution.py
@@ -6,18 +6,20 @@
 from jax.sharding import PartitionSpec as P
 
 W = 16
-CHUNKS = 1
+
+SENDS = (6, 2, 5, 1, 7, 3, 4)
+EVENTS = (-6, 2, -5, 1, 3, (0, 2, 1, 3), -7, 6, 5, 7, 4, (6, 5, 7, 4))
 
 epsilon = 1e-06
 
 MESH = pl.DeviceIdType.MESH
 
-PARTS = ((0, 24, "xyz"), (24, 48, "yzx"), (48, 64, "zxy"))
+PARTS = ((0, 24, "xyz"), (24, 40, "yzx"), (40, 64, "zxy"))
 
 
 def kernel(
-    x_ref, out_ref, win, snd, xb, inv_col, inv_row, pa, pb, pc, ra1, rb1, rc1, ra2, rb2, rc2, ra3, rb3, rc3,
-    load_sem, send_sem, recv_sem, pass_sem, passed_sem, out_sem, in_sem,
+    x_ref, out_ref, win, snd, mid, xb, inv_col, inv_row, pa, pb, pc, ra1, rb1, rc1, ra2, rb2, rc2, ra3, rb3, rc3,
+    load_sem, send_sem, recv_sem, mid_in, mid_out, pass_sem, passed_sem, out_sem, in_sem,
 ):
     band = lax.axis_index("band")
     chan = lax.axis_index("chan")
@@ -30,11 +32,13 @@
     bands, chips, cores, own, depth = xb.shape
     half = depth // 2
     tapers = half // W
-    step = bands // CHUNKS
 
     def device(x, y, z, core):
         return {"band": y * 2 + x % 2, "chan": ((x // 2) * 4 + z) * 2 + core}
 
+    def pick(table, j):
+        return sum(v * (1 - jnp.minimum(jnp.abs(j - n), 1)) for n, v in enumerate(table))
+
     def to_chip(i):
         return ((x_hi + i // 4) % 2) * 4 + (z + i % 4) % 4
 
@@ -47,9 +51,9 @@
     sibling = {"band": band, "chan": me * 2 + 1 - core}
 
     barrier = pltpu.get_barrier_semaphore()
-    peers = [same_group(to_chip(i)) for i in range(1, 8)] + [sibling]
-    peers += [device((x + o) % 4, y, z, core) for o in (1, 3)]
+    peers = [sibling] + [device((x + o) % 4, y, z, core) for o in (1, 2, 3)]
     peers += [device(x, (y + o) % 4, z, core) for o in (1, 2, 3)]
+    peers += [device(x, y, (z + o) % 4, core) for o in (1, 2, 3)]
     for peer in peers:
         pl.semaphore_signal(barrier, inc=1, device_id=peer, device_id_type=MESH)
 
@@ -58,7 +62,7 @@
         lanes = pl.ds(pl.multiple_of(chip * 128, 128), 128)
         return pltpu.make_async_copy(x_ref.at[:, :, :, lanes], win.at[i], load_sem.at[i])
 
-    for i in range(chips):
+    for i in SENDS + (0,):
         load(i).start()
 
     lane_band = lax.broadcasted_iota(jnp.int32, (16, 128), 1) // W
@@ -80,69 +84,104 @@
                 for b in range(bands):
                     put(b, r, part, v[b].astype(jnp.bfloat16))
 
+    def relayout(i):
+        load(i).wait()
+
+        def put(b, r, part, value):
+            snd[i, b, r : r + 16, part * half : (part + 1) * half] = value
+
+        transposed(i, put)
+
+    across = device((x + 2) % 4, y, z, core)
+
+    def along(dz):
+        return device(x, y, (z + dz) % 4, core)
+
+    def send(i):
+        return pltpu.make_async_remote_copy(
+            src_ref=snd.at[i],
+            dst_ref=xb.at[:, me, core],
+            send_sem=send_sem.at[i],
+            recv_sem=recv_sem.at[i],
+            device_id=device((x + 2 * (i // 4)) % 4, y, (z + i % 4) % 4, core),
+            device_id_type=MESH,
+        )
+
+    def to_mid(i):
+        return pltpu.make_async_remote_copy(
+            src_ref=snd.at[i],
+            dst_ref=mid.at[i - 4],
+            send_sem=send_sem.at[i],
+            recv_sem=mid_in.at[i - 4],
+            device_id=across,
+            device_id_type=MESH,
+        )
+
+    def from_mid(i):
+        return pltpu.make_async_remote_copy(
+            src_ref=mid.at[i - 4],
+            dst_ref=xb.at[:, (1 - x_hi) * 4 + z, core],
+            send_sem=mid_out.at[i - 4],
+            recv_sem=recv_sem.at[i],
+            device_id=along(i - 4),
+            device_id_type=MESH,
+        )
+
+    def landed(i):
+        return send(i) if i <= 4 else from_mid(i)
+
+    def forward(i):
+        chip = from_chip(i)
+        return pltpu.make_async_remote_copy(
+            src_ref=xb.at[:, chip, core],
+            dst_ref=xb.at[:, chip, core],
+            send_sem=pass_sem.at[i],
+            recv_sem=passed_sem.at[i],
+            device_id=sibling,
+            device_id_type=MESH,
+        )
+
+    relayout(SENDS[0])
+    pl.semaphore_wait(barrier, len(peers))
+    to_mid(SENDS[0]).start()
+
+    def relayout_and_send(j, carry):
+        i = pick(SENDS, j)
+        relayout(i)
+
+        @pl.when(i > 4)
+        def _():
+            to_mid(i).start()
+
+        @pl.when(i <= 4)
+        def _():
+            send(i).start()
+
+        return carry
+
+    lax.fori_loop(1, chips - 1, relayout_and_send, 0)
     load(0).wait()
 
     def put_own(b, r, part, value):
         xb[b, me, core, r : r + 16, part * half : (part + 1) * half] = value
 
     transposed(0, put_own)
-
-    def relayout(j, carry):
-        i = chips - 1 - j
-        load(i).wait()
-
-        def put(b, r, part, value):
-            snd[i, b, r : r + 16, part * half : (part + 1) * half] = value
-
-        transposed(i, put)
-        return carry
-
-    lax.fori_loop(0, chips - 1, relayout, 0)
-
-    def send(i, c):
-        return pltpu.make_async_remote_copy(
-            src_ref=snd.at[i, pl.ds(c * step, step)],
-            dst_ref=xb.at[pl.ds(c * step, step), me, core],
-            send_sem=send_sem.at[i, c],
-            recv_sem=recv_sem.at[i, c],
-            device_id=same_group(to_chip(i)),
-            device_id_type=MESH,
-        )
-
-    def forward(i, c):
-        chip = from_chip(i)
-        return pltpu.make_async_remote_copy(
-            src_ref=xb.at[pl.ds(c * step, step), chip, core],
-            dst_ref=xb.at[pl.ds(c * step, step), chip, core],
-            send_sem=pass_sem.at[i, c],
-            recv_sem=passed_sem.at[i, c],
-            device_id=sibling,
-            device_id_type=MESH,
-        )
-
-    pl.semaphore_wait(barrier, len(peers))
-    for c in range(CHUNKS):
-        def start_send(j, carry):
-            send(chips - 1 - j, c).start()
-            return carry
-
-        lax.fori_loop(0, chips - 1, start_send, 0)
-        forward(0, c).start()
+    forward(0).start()
 
     lane = lax.broadcasted_iota(jnp.int32, (2 * own, 128), 1)
 
-    def normalise(i, c):
-        forward(i, c).wait_recv()
+    def normalise(i):
+        forward(i).wait_recv()
         chip = from_chip(i)
         power = jnp.ones((2 * own, 128), jnp.float32)
-        for b in range(step):
-            v = xb[c * step + b, chip].reshape(2 * own, depth).astype(jnp.float32)
+        for b in range(bands):
+            v = xb[b, chip].reshape(2 * own, depth).astype(jnp.float32)
             v = v * v
             total = jnp.sum(v[:, :half] + v[:, half:], axis=1, keepdims=True) + epsilon
             power = jnp.where(lane == b, total, power)
         inverse = 1.0 / power
-        inv_col[c, pl.ds(pl.multiple_of(chip * 2 * own, 128), 2 * own), :] = inverse
-        inv_row[c, :, pl.ds(pl.multiple_of(chip * 128, 128), 128)] = inverse.T[:8, :]
+        inv_col[pl.ds(pl.multiple_of(chip * 2 * own, 128), 2 * own), :] = inverse
+        inv_row[:, pl.ds(pl.multiple_of(chip * 128, 128), 128)] = inverse.T[:8, :]
 
     contract = (((1,), (1,)), ((), ()))
     stores = ((pa, 0), (pb, 1), (pc, 2))
@@ -172,24 +211,28 @@
             device_id_type=MESH,
         )
 
-    def follow(j):
-        return (chips - j) % chips
-
-    def arrive(j, carry):
-        i = follow(j)
-        send(i, 0).wait_recv()
-        forward(i, 0).start()
-        normalise(follow(j - 1), 0)
-        return carry
-
-    lax.fori_loop(1, chips, arrive, 0)
-    normalise(1, 0)
+    def group(items):
+        def one(j, carry):
+            normalise(pick(items, j))
+            return carry
+
+        lax.fori_loop(0, len(items), one, 0)
+
+    for event in EVENTS:
+        if isinstance(event, tuple):
+            group(event)
+        elif event < 0:
+            to_mid(-event).wait_recv()
+            from_mid(-event).start()
+        else:
+            landed(event).wait_recv()
+            forward(event).start()
 
     def tile(t, carry):
         row = (x_hi + 1 + t // 4) % 2
         col = (y + 2 + 3 * (t % 4)) % 4
         acc = jnp.zeros((256, 256), jnp.float32)
-        scale_row = inv_row[0, :, pl.ds(pl.multiple_of(col * 256, 256), 256)]
+        scale_row = inv_row[:, pl.ds(pl.multiple_of(col * 256, 256), 256)]
         for b in range(bands):
             left = xb[b, pl.ds(row * 4, 4), core].reshape(256, depth)
             right = xb[b, pl.ds(col * 2, 2)].reshape(256, depth)
@@ -198,7 +241,7 @@
             im = lax.dot_general(turned, right, contract, preferred_element_type=jnp.float32)
             rows = jnp.concatenate(
                 [
-                    inv_col[0, pl.ds(pl.multiple_of((row * 4 + q) * 128 + core * own, own), own), b : b + 1]
+                    inv_col[pl.ds(pl.multiple_of((row * 4 + q) * 128 + core * own, own), own), b : b + 1]
                     for q in range(4)
                 ],
                 axis=0,
@@ -249,14 +292,12 @@
         for phase in range(3):
             for o in (1, 2, 3):
                 hop(n, phase, o).wait_send()
-    for c in range(CHUNKS):
-        def finish(i, carry):
-            send(i, c).wait_send()
-            forward(i, c).wait_send()
-            return carry
-
-        lax.fori_loop(1, chips, finish, 0)
-        forward(0, c).wait_send()
+    for i in range(1, 8):
+        (to_mid(i) if i > 4 else send(i)).wait_send()
+        forward(i).wait_send()
+        if i > 4:
+            from_mid(i).wait_send()
+    forward(0).wait_send()
 
 
 def body(coeffs):
@@ -270,9 +311,10 @@
     scratch = [
         pltpu.VMEM((chips, parts, tapers, own, 128), bf16),
         pltpu.VMEM((chips, bands, own, depth), bf16),
+        pltpu.VMEM((4, bands, own, depth), bf16),
         pltpu.VMEM((bands, chips, 2, own, depth), bf16),
-        pltpu.VMEM((CHUNKS, chips * 2 * own, 128), f32),
-        pltpu.VMEM((CHUNKS, 8, chips * 2 * own), f32),
+        pltpu.VMEM((chips * 2 * own, 128), f32),
+        pltpu.VMEM((8, chips * 2 * own), f32),
     ]
     scratch += [pltpu.VMEM((4, 4, 4, r, 128), f32) for r in rows]
     scratch += [pltpu.VMEM((3, 4, 4, r, 128), f32) for r in rows]
@@ -280,10 +322,12 @@
     scratch += [pltpu.VMEM((3, r, 128), f32) for r in rows]
     scratch += [
         pltpu.SemaphoreType.DMA((chips,)),
-        pltpu.SemaphoreType.DMA((chips, CHUNKS)),
-        pltpu.SemaphoreType.DMA((chips, CHUNKS)),
-        pltpu.SemaphoreType.DMA((chips, CHUNKS)),
-        pltpu.SemaphoreType.DMA((chips, CHUNKS)),
+        pltpu.SemaphoreType.DMA((chips,)),
+        pltpu.SemaphoreType.DMA((chips,)),
+        pltpu.SemaphoreType.DMA((4,)),
+        pltpu.SemaphoreType.DMA((4,)),
+        pltpu.SemaphoreType.DMA((chips,)),
+        pltpu.SemaphoreType.DMA((chips,)),
         pltpu.SemaphoreType.DMA((3, 3, 4)),
         pltpu.SemaphoreType.DMA((3, 3, 4)),
     ]

time: 60 us -> 56.3 us (0.938)
  Pallas kernels: 59.3 us -> 55.6 us
    pallas_call x1, Pallas kernels: 59.3 us -> 55.6 us  [body(): pl.pallas_call(kernel, out_shape=jax.ShapeDtypeStruct((own, 128), f32), i...]
where the time goes in v4:
time: 56.3 us; the launch traced here: 56.2 us
  Pallas kernels  55.6 us (99%)
  local copies, waits for them, and re-layouts  0.62 us (1%)
    pallas_call x1, Pallas kernels, body(): pl.pallas_call(kernel, out_shape=jax.ShapeDtypeStruct((own, 128), f32), i...  55.6 us

profile of v4, /device:TPU:0, one launch (start us, length us, event | category | flops | bytes accessed | tf_op | source)
XLA Modules:
  0.0 56.2 jit_solution(18019437775321395112)
XLA Ops:
  0.0 55.6 %shard_map.17 = f32[64,128]{1,0:T(8,128)S(1)} custom-call(bf16[2,8,64,1024]{3,2,1,0:T(8,128)(2,1)} %x_ref.1), custom_call_target="tpu_custom_call" | custom-call | tf_op jit(solution)/shard_map/pallas_call | solution.py:334
  55.6 0.6 %copy.3 = f32[64,128]{1,0:T(8,128)} copy(f32[64,128]{1,0:T(8,128)S(1)} %shard_map.17) | data formatting | bytes 65536

commit v5 on v4

--- a/solution.py
+++ b/solution.py
@@ -50,20 +50,20 @@
 
     sibling = {"band": band, "chan": me * 2 + 1 - core}
 
+    def load(i):
+        chip = to_chip(i)
+        lanes = pl.ds(pl.multiple_of(chip * 128, 128), 128)
+        return pltpu.make_async_copy(x_ref.at[:, :, :, lanes], win.at[i], load_sem.at[i])
+
+    for i in SENDS + (0,):
+        load(i).start()
+
     barrier = pltpu.get_barrier_semaphore()
-    peers = [sibling] + [device((x + o) % 4, y, z, core) for o in (1, 2, 3)]
+    peers = [device((x + o) % 4, y, z, core) for o in (2, 1, 3)] + [sibling]
     peers += [device(x, (y + o) % 4, z, core) for o in (1, 2, 3)]
     peers += [device(x, y, (z + o) % 4, core) for o in (1, 2, 3)]
     for peer in peers:
         pl.semaphore_signal(barrier, inc=1, device_id=peer, device_id_type=MESH)
-
-    def load(i):
-        chip = to_chip(i)
-        lanes = pl.ds(pl.multiple_of(chip * 128, 128), 128)
-        return pltpu.make_async_copy(x_ref.at[:, :, :, lanes], win.at[i], load_sem.at[i])
-
-    for i in SENDS + (0,):
-        load(i).start()
 
     lane_band = lax.broadcasted_iota(jnp.int32, (16, 128), 1) // W
 

time: 56.3 us -> 56.5 us (level)
  no operation moved by 1% of the time
where the time goes in v5:
time: 56.5 us; the launch traced here: 56.3 us
  Pallas kernels  55.7 us (99%)
  local copies, waits for them, and re-layouts  0.62 us (1%)
    pallas_call x1, Pallas kernels, body(): pl.pallas_call(kernel, out_shape=jax.ShapeDtypeStruct((own, 128), f32), i...  55.7 us

profile of v5, /device:TPU:0, one launch (start us, length us, event | category | flops | bytes accessed | tf_op | source)
XLA Modules:
  0.0 56.3 jit_solution(321251223108081001)
XLA Ops:
  0.0 55.7 %shard_map.17 = f32[64,128]{1,0:T(8,128)S(1)} custom-call(bf16[2,8,64,1024]{3,2,1,0:T(8,128)(2,1)} %x_ref.1), custom_call_target="tpu_custom_call" | custom-call | tf_op jit(solution)/shard_map/pallas_call | solution.py:334
  55.7 0.6 %copy.3 = f32[64,128]{1,0:T(8,128)} copy(f32[64,128]{1,0:T(8,128)S(1)} %shard_map.17) | data formatting | bytes 65536

commit v6 on v4

--- a/solution.py
+++ b/solution.py
@@ -267,7 +267,12 @@
             hop(2, 0, o, (pl.ds(row * 2, 2), col)).start()
         return carry
 
-    lax.fori_loop(0, 8, tile, 0)
+    def two_tiles(t, carry):
+        tile(2 * t, 0)
+        tile(2 * t + 1, 0)
+        return carry
+
+    lax.fori_loop(0, 4, two_tiles, 0)
 
     for phase in range(3):
         for n in range(3):

time: 56.3 us -> 56.3 us (level)
  no operation moved by 1% of the time
where the time goes in v6:
time: 56.3 us; the launch traced here: 56.2 us
  Pallas kernels  55.6 us (99%)
  local copies, waits for them, and re-layouts  0.62 us (1%)
    pallas_call x1, Pallas kernels, body(): pl.pallas_call(kernel, out_shape=jax.ShapeDtypeStruct((own, 128), f32), i...  55.6 us

profile of v6, /device:TPU:0, one launch (start us, length us, event | category | flops | bytes accessed | tf_op | source)
XLA Modules:
  0.0 56.2 jit_solution(16615962941547147186)
XLA Ops:
  0.0 55.6 %shard_map.17 = f32[64,128]{1,0:T(8,128)S(1)} custom-call(bf16[2,8,64,1024]{3,2,1,0:T(8,128)(2,1)} %x_ref.1), custom_call_target="tpu_custom_call" | custom-call | tf_op jit(solution)/shard_map/pallas_call | solution.py:339
  55.6 0.6 %copy.3 = f32[64,128]{1,0:T(8,128)} copy(f32[64,128]{1,0:T(8,128)S(1)} %shard_map.17) | data formatting | bytes 65536
